TPU v7x, 8 devices: a whole 2x2x1 slice. The times are simulated.
8 devices in a mesh: dp: 2 (over z, y), tp: 4 (over x, core).
Axes of the slice: x: 2, y: 2, z: 1, core: 2. Of those that a mesh axis runs over, the one named last changes fastest.
Arguments:
- x_in: bfloat16 [16384, 2048], P(('dp', 'tp')), parts along dimension 0
- w_in: bfloat16 [2048, 16384], P(None, 'tp')
- grad_out: bfloat16 [16384, 16384], P('dp', 'tp'), parts along dimension 0
Outputs:
- output 1: bfloat16 [16384, 2048], P(('dp', 'tp')), parts along dimension 0
- output 2: float32 [4096, 16384], P('dp', 'tp'), parts along dimension 0
There are 2 independent parts. A program takes and returns all parts, laid end to end along the dimension named above; an argument that names none is the same for every part.
All inputs are finite; a program needn't handle non-finite values.
Results may differ from a plain program's by a relative error of at most 0.001.
Values are sent between devices in bfloat16 or wider.
A program may use at most 1 GiB of HBM per device.

v0:
```python
import jax
import jax.numpy as jnp
from jax import lax
from jax.sharding import PartitionSpec as P


def solution(mesh):
    def per_device(x_blk, w_blk, grad_blk):
        x_full = lax.all_gather(x_blk, "tp", axis=0, tiled=True)
        part_dx = lax.dot_general(grad_blk, w_blk, (((1,), (1,)), ((), ())), preferred_element_type=jnp.float32)
        grad_x = lax.psum_scatter(part_dx, "tp", scatter_dimension=0, tiled=True).astype(jnp.bfloat16)
        grad_w = lax.dot_general(x_full, grad_blk, (((0,), (0,)), ((), ())), preferred_element_type=jnp.float32)
        return grad_x, grad_w

    return jax.shard_map(
        per_device,
        mesh=mesh,
        in_specs=(P(("dp", "tp"), None), P(None, "tp"), P("dp", "tp")),
        out_specs=(P(("dp", "tp"), None), P("dp", "tp")),
        check_vma=False,
    )
```

profile of v0, /device:TPU:0, one launch (start us, length us, event | category | flops | bytes accessed | tf_op | source)
XLA Modules:
  0.0 670.7 jit_solution(14943299669840305332)
XLA Ops:
  7.2 0.0 all-gather.2.cloned.1.call-start
  7.2 0.7 all-gather.2.cloned.1.call-update
  7.9 0.0 reduce-scatter.4.cloned.1.call-start
  7.9 149.5 %fusion = f32[8192,2048]{1,0:T(8,128)} fusion(bf16[8192,4096]{1,0:T(8,128)(2,1)} %param.5, bf16[2048,4096]{1,0:T(8,128)(2,1)} %param.4), kind=kOutput, calls=%fused_computation | convolution fusion | flops 137438953472 | bytes 150994944 | tf_op jit(solution)/shard_map/dot_general | solution.py:10
  157.4 0.0 reduce-scatter.4.cloned.1.call-update
  157.4 54.3 %all-gather.2.cloned.1.call-done = bf16[8192,2048]{1,0:T(8,128)(2,1)} async-done(((bf16[2048,2048]{1,0:T(8,128)(2,1)}), bf16[8192,2048]{1,0:T(8,128)(2,1)}) %all-gather.2.cloned.1.call-update) | async-done | bytes 33554448 | tf_op jit(solution)/shard_map/all_gather | solution.py:9
  211.7 157.8 %fusion.1 = f32[2048,4096]{1,0:T(8,128)} fusion(bf16[8192,2048]{1,0:T(8,128)(2,1)} %all-gather.2.cloned.1.call-done, bf16[8192,4096]{1,0:T(8,128)(2,1)} %param.5), kind=kOutput, calls=%fused_computation.1 | convolution fusion | flops 137438953472 | bytes 134217728 | tf_op jit(solution)/shard_map/dot_general | solution.py:12
  369.6 285.3 %reduce-scatter.4.cloned.1.call-done = f32[2048,2048]{1,0:T(8,128)} async-done(((f32[8192,2048]{1,0:T(8,128)}), f32[2048,2048]{1,0:T(8,128)}) %reduce-scatter.4.cloned.1.call-update) | async-done | bytes 16777232
  654.9 9.0 %convert_element_type.3 = bf16[2048,2048]{1,0:T(8,128)(2,1)} convert(f32[2048,2048]{1,0:T(8,128)} %reduce-scatter.4.cloned.1.call-done) | non-fusion elementwise | flops 4194304 | bytes 25165824 | tf_op jit(solution)/shard_map/convert_element_type | solution.py:11
Async XLA Ops:
  7.2 204.6 %all-gather.2.cloned.1.call-start = ((), (), s32[]{:S(2)}) async-start(), calls=%async_computation.1 | async-start | bytes 41943040 | tf_op jit(solution)/shard_map/all_gather | solution.py:9
  7.9 647.0 %reduce-scatter.4.cloned.1.call-start = ((), (), s32[]{:S(2)}) async-start(), calls=%async_computation.2 | async-start | bytes 83886080
Sparse Core Ops, SparseCore 0:
  9.5 202.1 all-gather.1
  214.3 440.5 reduce-scatter.3
where the time goes:
time: 671 us
  waiting for transfers between devices  340 us (51%)
  matrix products  307 us (46%)
  between operations  14 us (2%)
  other arithmetic  9.05 us (1%)
    unnamed x3, waiting for transfers between devices  286 us
    dot_general x1, matrix products, per_device(): lax.dot_general(x_full, grad_blk, (((0,), (0,)), ((), ())), preferred_ele...  158 us
    dot_general x1, matrix products, per_device(): lax.dot_general(grad_blk, w_blk, (((1,), (1,)), ((), ())), preferred_elem...  149 us
    all_gather x1, waiting for transfers between devices, per_device(): x_full = lax.all_gather(x_blk, 'tp', axis=0, tiled=True)  54.3 us
  transfers between devices with their start and end apart: 2, of which 2 were waited for; matrix products, arithmetic and copies ran while one was open for 46% of the time, Pallas kernels for 0%

commit v1 on v0

v1 whole, which is shorter than its diff:
```python
import jax
import jax.numpy as jnp
from jax import lax
from jax.sharding import PartitionSpec as P


CHUNKS = (1536, 384, 96, 32)


def solution(mesh):
    tp_size = mesh.shape["tp"]
    sib_perm = [(t, t ^ 1) for t in range(tp_size)]
    peer_perm = [(t, t ^ 2) for t in range(tp_size)]

    def permute(value, perm):
        return lax.ppermute(value, "tp", perm)

    def half(value, core, rows):
        return lax.dynamic_slice_in_dim(value, core * rows, rows, 0, allow_negative_indices=False)

    def pair(mine, other, core):
        first = jnp.where(core == 0, mine, other)
        second = jnp.where(core == 0, other, mine)
        return jnp.concatenate((first, second), axis=0)

    def per_device(x_blk, w_blk, grad_blk):
        rows = x_blk.shape[0]
        me = lax.axis_index("tp")
        chip, core = me >> 1, me & 1

        def chip_rows(grad, which):
            return lax.dynamic_slice_in_dim(grad, which * 2 * rows, 2 * rows, 0, allow_negative_indices=False)

        def partial(grad, which):
            return lax.dot_general(
                chip_rows(grad, which), w_blk, (((1,), (1,)), ((), ())),
                preferred_element_type=jnp.float32)

        def weight_term(x_rows, grad, which):
            return lax.dot_general(
                x_rows, chip_rows(grad, which), (((0,), (0,)), ((), ())),
                preferred_element_type=jnp.float32)

        x_peer = permute(x_blk, peer_perm)
        x_sib = permute(x_blk, sib_perm)
        x_opp = permute(x_peer, sib_perm)

        remote = partial(grad_blk, chip ^ 1)
        from_sib = permute(half(remote, core ^ 1, rows), sib_perm)
        chip_sum = half(remote, core, rows) + from_sib
        arrived, start = [], 0
        for size in CHUNKS:
            arrived.append(permute(chip_sum[start:start + size], peer_perm))
            start += size

        grad_late, _ = lax.optimization_barrier((grad_blk, chip_sum))
        local = partial(grad_late, chip)
        own = half(local, core, rows) + permute(half(local, core ^ 1, rows), sib_perm)

        grad_w = weight_term(pair(x_blk, x_sib, core), grad_late, chip)
        grad_w = grad_w + weight_term(pair(x_peer, x_opp, core), grad_late, chip ^ 1)

        grad_x, start = jnp.zeros(x_blk.shape, jnp.bfloat16), 0
        for size, part in zip(CHUNKS, arrived):
            done = (own[start:start + size] + part).astype(jnp.bfloat16)
            grad_x = lax.dynamic_update_slice_in_dim(grad_x, done, start, 0)
            start += size
        return grad_x, grad_w

    return jax.shard_map(
        per_device,
        mesh=mesh,
        in_specs=(P(("dp", "tp"), None), P(None, "tp"), P("dp", "tp")),
        out_specs=(P(("dp", "tp"), None), P("dp", "tp")),
        check_vma=False,
    )
```

time: 671 us -> 689 us (1.027)
  waiting for transfers between devices: 340 us -> 232 us
  other arithmetic: 9.05 us -> 65.8 us
  local copies, waits for them, and re-layouts: 0 us -> 52.3 us
  matrix products: 307 us -> 329 us
  between operations: 14 us -> 0.7 us
  starting transfers between devices: 0.08 us -> 7.83 us
    unnamed x3 -> x0, waiting for transfers between devices: 286 us -> none
    ppermute x0 -> x9, waiting for transfers between devices: none -> 232 us  [permute(): return lax.ppermute(value, 'tp', perm)]
    all_gather x1 -> x0, waiting for transfers between devices: 54.3 us -> none  [per_device(): x_full = lax.all_gather(x_blk, 'tp', axis=0, tiled=True)]
    add x0 -> x2, other arithmetic: none -> 29.1 us  [the longest x1 17.4 us: per_device(): chip_sum = half(remote, core, rows) + from_sib]
    dynamic_slice x0 -> x2, local copies, waits for them, and re-layouts: none -> 23.3 us  [half(): lax.dynamic_slice_in_dim(value, core * rows, rows, 0, allow_negative_indi...]
    select_n x0 -> x2, other arithmetic: none -> 22.8 us  [pair(): first = jnp.where(core == 0, mine, other)]
    dot_general x2 -> x4, matrix products: 307 us -> 329 us  [the longest x2 171 us: weight_term(): lax.dot_general(x_rows, chip_rows(grad, which), (((0,), (0,)), ((), ())),...]
    slice x0 -> x4, local copies, waits for them, and re-layouts: none -> 18.9 us  [per_device(): arrived.append(permute(chip_sum[start:start + size], peer_perm))]
  transfers between devices with their start and end apart: 2 -> 9, of which waited for: 2 -> 4; matrix products, arithmetic and copies ran while one was open for 46% -> 51% of each run, Pallas kernels for 0% -> 0%
where the time goes in v1:
time: 689 us; the launch traced here: 688 us
  matrix products  329 us (48%)
  waiting for transfers between devices  232 us (34%)
  other arithmetic  65.8 us (10%)
  local copies, waits for them, and re-layouts  52.3 us (8%)
  starting transfers between devices  7.83 us (1%)
    ppermute x9, waiting for transfers between devices, permute(): return lax.ppermute(value, 'tp', perm)  232 us
    dot_general x2, matrix products, weight_term(): lax.dot_general(x_rows, chip_rows(grad, which), (((0,), (0,)), ((), ())),...  171 us
    dot_general x2, matrix products, partial(): lax.dot_general(chip_rows(grad, which), w_blk, (((1,), (1,)), ((), ())),...  158 us
    dynamic_slice x2, local copies, waits for them, and re-layouts, half(): lax.dynamic_slice_in_dim(value, core * rows, rows, 0, allow_negative_indi...  23.3 us
    select_n x2, other arithmetic, pair(): first = jnp.where(core == 0, mine, other)  22.8 us
    slice x4, local copies, waits for them, and re-layouts, per_device(): arrived.append(permute(chip_sum[start:start + size], peer_perm))  18.9 us
    add x1, other arithmetic, per_device(): chip_sum = half(remote, core, rows) + from_sib  17.4 us
  transfers between devices with their start and end apart: 9, of which 4 were waited for; matrix products, arithmetic and copies ran while one was open for 51% of the time, Pallas kernels for 0%

profile of v1, /device:TPU:0, one launch (start us, length us, event | category | flops | bytes accessed | tf_op | source)
XLA Modules:
  0.0 688.2 jit_solution(17688638527466568203)
XLA Ops:
  0.6 78.9 %fusion.2 = f32[4096,2048]{1,0:T(8,128)} fusion(bf16[2048,4096]{1,0:T(8,128)(2,1)} %param.4, bf16[8192,4096]{1,0:T(8,128)(2,1)} %param.5, s32[]{:T(128)S(6)} %mul.8), kind=kOutput, calls=%fused_computation.2 | convolution fusion | flops 68719476736 | bytes 83886080 | tf_op jit(solution)/shard_map/dot_general | solution.py:35
  79.6 11.6 %constant_dynamic-slice_fusion.1 = f32[2048,2048]{1,0:T(8,128)} fusion(f32[4096,2048]{1,0:T(8,128)} %fusion.2, s32[]{:T(128)S(6)} %mul.10), kind=kLoop, calls=%fused_computation.36 | loop fusion | bytes 33554436 | tf_op jit(solution)/shard_map/dynamic_slice | solution.py:19
  91.2 0.8 collective-permute-start
  92.0 2.5 collective-permute-start.7
  94.5 0.2 collective-permute-start.6
  94.7 181.2 %collective-permute-done.7 = bf16[2048,2048]{1,0:T(8,128)(2,1)} collective-permute-done((bf16[2048,2048]{1,0:T(8,128)(2,1)}, bf16[2048,2048]{1,0:T(8,128)(2,1)}, u32[]{:S(2)}, u32[]{:S(2)}) %collective-permute-start.7) | collective-permute-done | bytes 8388640 | tf_op jit(solution)/shard_map/ppermute | solution.py:16
  275.9 0.0 collective-permute-start.8
  275.9 0.0 collective-permute-done.6
  275.9 11.4 %broadcast_select_fusion.3 = (bf16[2048,2048]{1,0:T(8,128)(2,1)}, bf16[2048,2048]{1,0:T(8,128)(2,1)}) fusion(bf16[2048,2048]{1,0:T(8,128)(2,1)} %param.3, bf16[2048,2048]{1,0:T(8,128)(2,1)} %collective-permute-done.6, pred[]{:T(512)S(6)} %eq.2), kind=kLoop, calls=%fused_computation.22 | loop fusion | flops 8388608 | bytes 33554432 | tf_op jit(solution)/shard_map/jit(_where)/select_n | solution.py:22
  287.4 0.0 collective-permute-done
  287.4 17.4 %dynamic-slice_add_fusion.1 = f32[2048,2048]{1,0:T(8,128)} fusion(f32[2048,2048]{1,0:T(8,128)} %collective-permute-done, f32[4096,2048]{1,0:T(8,128)} %fusion.2, s32[]{:T(128)S(6)} %mul.9), kind=kLoop, calls=%fused_computation.16 | loop fusion | flops 4194304 | bytes 50331652 | tf_op jit(solution)/shard_map/add | solution.py:50
  304.8 11.3 %slice.33 = f32[1536,2048]{1,0:T(8,128)} slice(f32[2048,2048]{1,0:T(8,128)} %dynamic-slice_add_fusion.1), slice={[0:1536], [0:2048]} | slice | bytes 25165824 | tf_op jit(solution)/shard_map/slice | solution.py:53
  316.1 3.9 slice.35
  320.0 2.1 slice.37
  322.0 1.7 slice.39
  323.7 1.7 collective-permute-start.2
  325.4 79.0 %fusion.6 = f32[4096,2048]{1,0:T(8,128)} fusion(bf16[2048,4096]{1,0:T(8,128)(2,1)} %param.4, bf16[8192,4096]{1,0:T(8,128)(2,1)} %param.5, s32[]{:T(128)S(6)} %mul.11), kind=kOutput, calls=%fused_computation.6 | convolution fusion | flops 68719476736 | bytes 83886080 | tf_op jit(solution)/shard_map/dot_general | solution.py:35
  404.4 11.6 %constant_dynamic-slice_fusion = f32[2048,2048]{1,0:T(8,128)} fusion(f32[4096,2048]{1,0:T(8,128)} %fusion.6, s32[]{:T(128)S(6)} %mul.10), kind=kLoop, calls=%fused_computation.34 | loop fusion | bytes 33554436 | tf_op jit(solution)/shard_map/dynamic_slice | solution.py:19
  416.0 0.1 collective-permute-start.1
  416.2 0.4 collective-permute-start.3
  416.5 1.7 collective-permute-start.4
  418.2 0.0 copy-start.1
  418.2 80.6 %fusion.4 = f32[2048,4096]{1,0:T(8,128)} fusion(bf16[8192,4096]{1,0:T(8,128)(2,1)} %param.5, s32[]{:T(128)S(6)} %mul.11, bf16[2048,2048]{1,0:T(8,128)(2,1)} %get-tuple-element.7, bf16[2048,2048]{1,0:T(8,128)(2,1)} %get-tuple-element.6), kind=kOutput, calls=%fused_computation.4 | convolution fusion | flops 68753031168 | bytes 83886080 | tf_op jit(solution)/shard_map/dot_general | solution.py:40
  498.8 0.0 collective-permute-done.8
  498.9 0.0 copy-done.1
  498.9 0.4 collective-permute-start.5
  499.2 11.4 %broadcast_select_fusion.1 = (bf16[2048,2048]{1,0:T(8,128)(2,1)}, bf16[2048,2048]{1,0:T(8,128)(2,1)}) fusion(bf16[2048,2048]{1,0:T(8,128)(2,1)} %collective-permute-done.7, bf16[2048,2048]{1,0:T(8,128)(2,1)} %collective-permute-done.8, pred[]{:T(512)S(6)} %eq.2), kind=kLoop, calls=%fused_computation.20 | loop fusion | flops 8388608 | bytes 33554432 | tf_op jit(solution)/shard_map/jit(_where)/select_n | solution.py:22
  510.6 90.5 %fusion.8 = f32[2048,4096]{1,0:T(8,128)} fusion(f32[2048,4096]{1,0:T(8,128)} %fusion.4, bf16[8192,4096]{1,0:T(8,128)(2,1)} %param.5, s32[]{:T(128)S(6)} %mul.8, bf16[2048,2048]{1,0:T(8,128)(2,1)} %get-tuple-element.5, bf16[2048,2048]{1,0:T(8,128)(2,1)} %get-tuple-element.4), kind=kOutput, calls=%fused_computation.8 | convolution fusion | flops 68761419776 | bytes 117440512 | tf_op jit(solution)/shard_map/dot_general | solution.py:40
  601.1 0.0 collective-permute-done.1
  601.1 11.6 %dynamic-slice_add_fusion = f32[2048,2048]{1,0:T(8,128)S(1)} fusion(f32[2048,2048]{1,0:T(8,128)} %collective-permute-done.1, f32[4096,2048]{1,0:T(8,128)} %fusion.6, s32[]{:T(128)S(6)} %mul.9), kind=kLoop, calls=%fused_computation.15 | loop fusion | flops 4194304 | bytes 50331652 | tf_op jit(solution)/shard_map/add | solution.py:58
  612.8 0.0 copy-start
  612.8 0.0 collective-permute-done.2
  612.8 5.7 copy-done
  618.5 5.7 fusion.17
  624.2 4.5 dynamic_update_slice.12
  628.7 35.9 %collective-permute-done.3 = f32[384,2048]{1,0:T(8,128)} collective-permute-done((f32[384,2048]{1,0:T(8,128)}, f32[384,2048]{1,0:T(8,128)}, u32[]{:S(2)}, u32[]{:S(2)}) %collective-permute-start.3) | collective-permute-done | bytes 3145760 | tf_op jit(solution)/shard_map/ppermute | solution.py:16
  664.6 4.4 fusion.19
  669.0 12.4 %collective-permute-done.4 = f32[96,2048]{1,0:T(8,128)} collective-permute-done((f32[96,2048]{1,0:T(8,128)}, f32[96,2048]{1,0:T(8,128)}, u32[]{:S(2)}, u32[]{:S(2)}) %collective-permute-start.4) | collective-permute-done | bytes 786464 | tf_op jit(solution)/shard_map/ppermute | solution.py:16
  681.5 2.2 fusion.21
  683.7 2.9 collective-permute-done.5
  686.5 1.6 fusion.23
Async XLA Ops:
  91.2 196.2 %collective-permute-start = (f32[2048,2048]{1,0:T(8,128)}, f32[2048,2048]{1,0:T(8,128)}, u32[]{:S(2)}, u32[]{:S(2)}) collective-permute-start(f32[2048,2048]{1,0:T(8,128)} %constant_dynamic-slice_fusion.1), channel_id=1, source_target_pairs={{0,1},{1,0},{2,3},{3,2},{4,5},{5,4},{6,7},{7,6}} | collective-permute-start | bytes 50331656 | tf_op jit(solution)/shard_map/ppermute | solution.py:16
  92.0 183.9 %collective-permute-start.7 = (bf16[2048,2048]{1,0:T(8,128)(2,1)}, bf16[2048,2048]{1,0:T(8,128)(2,1)}, u32[]{:S(2)}, u32[]{:S(2)}) collective-permute-start(bf16[2048,2048]{1,0:T(8,128)(2,1)} %param.3), channel_id=1, source_target_pairs={{0,2},{1,3},{2,0},{3,1},{4,6},{5,7},{6,4},{7,5}} | collective-permute-start | bytes 25165832 | tf_op jit(solution)/shard_map/ppermute | solution.py:16
  94.5 181.4 %collective-permute-start.6 = (bf16[2048,2048]{1,0:T(8,128)(2,1)}, bf16[2048,2048]{1,0:T(8,128)(2,1)}, u32[]{:S(2)}, u32[]{:S(2)}) collective-permute-start(bf16[2048,2048]{1,0:T(8,128)(2,1)} %param.3), channel_id=1, source_target_pairs={{0,1},{1,0},{2,3},{3,2},{4,5},{5,4},{6,7},{7,6}} | collective-permute-start | bytes 25165832 | tf_op jit(solution)/shard_map/ppermute | solution.py:16
  275.9 222.9 %collective-permute-start.8 = (bf16[2048,2048]{1,0:T(8,128)(2,1)}, bf16[2048,2048]{1,0:T(8,128)(2,1)}, u32[]{:S(2)}, u32[]{:S(2)}) collective-permute-start(bf16[2048,2048]{1,0:T(8,128)(2,1)} %collective-permute-done.7), channel_id=1, source_target_pairs={{0,1},{1,0},{2,3},{3,2},{4,5},{5,4},{6,7},{7,6}} | collective-permute-start | bytes 25165832 | tf_op jit(solution)/shard_map/ppermute | solution.py:16
  323.7 289.1 %collective-permute-start.2 = (f32[1536,2048]{1,0:T(8,128)}, f32[1536,2048]{1,0:T(8,128)}, u32[]{:S(2)}, u32[]{:S(2)}) collective-permute-start(f32[1536,2048]{1,0:T(8,128)} %slice.33), channel_id=1, source_target_pairs={{0,2},{1,3},{2,0},{3,1},{4,6},{5,7},{6,4},{7,5}} | collective-permute-start | bytes 37748744 | tf_op jit(solution)/shard_map/ppermute | solution.py:16
  416.0 185.1 %collective-permute-start.1 = (f32[2048,2048]{1,0:T(8,128)}, f32[2048,2048]{1,0:T(8,128)}, u32[]{:S(2)}, u32[]{:S(2)}) collective-permute-start(f32[2048,2048]{1,0:T(8,128)} %constant_dynamic-slice_fusion), channel_id=1, source_target_pairs={{0,1},{1,0},{2,3},{3,2},{4,5},{5,4},{6,7},{7,6}} | collective-permute-start | bytes 50331656 | tf_op jit(solution)/shard_map/ppermute | solution.py:16
  416.2 248.5 %collective-permute-start.3 = (f32[384,2048]{1,0:T(8,128)}, f32[384,2048]{1,0:T(8,128)}, u32[]{:S(2)}, u32[]{:S(2)}) collective-permute-start(f32[384,2048]{1,0:T(8,128)} %slice.35), channel_id=1, source_target_pairs={{0,2},{1,3},{2,0},{3,1},{4,6},{5,7},{6,4},{7,5}} | collective-permute-start | bytes 9437192 | tf_op jit(solution)/shard_map/ppermute | solution.py:16
  416.5 264.9 %collective-permute-start.4 = (f32[96,2048]{1,0:T(8,128)}, f32[96,2048]{1,0:T(8,128)}, u32[]{:S(2)}, u32[]{:S(2)}) collective-permute-start(f32[96,2048]{1,0:T(8,128)} %slice.37), channel_id=1, source_target_pairs={{0,2},{1,3},{2,0},{3,1},{4,6},{5,7},{6,4},{7,5}} | collective-permute-start | bytes 2359304 | tf_op jit(solution)/shard_map/ppermute | solution.py:16
  418.2 80.7 %copy-start.1 = (f32[32,2048]{1,0:T(8,128)S(1)}, f32[32,2048]{1,0:T(8,128)}, u32[]{:S(2)}) copy-start(f32[32,2048]{1,0:T(8,128)} %slice.39) | copy-start | bytes 786436
  498.9 187.7 %collective-permute-start.5 = (f32[32,2048]{1,0:T(8,128)S(1)}, f32[32,2048]{1,0:T(8,128)S(1)}, u32[]{:S(2)}, u32[]{:S(2)}) collective-permute-start(f32[32,2048]{1,0:T(8,128)S(1)} %copy-done.1), channel_id=1, source_target_pairs={{0,2},{1,3},{2,0},{3,1},{4,6},{5,7},{6,4},{7,5}} | collective-permute-start | bytes 786440 | tf_op jit(solution)/shard_map/ppermute | solution.py:16
  612.8 5.7 copy-start

commit v2 on v1

--- a/solution.py
+++ b/solution.py
@@ -47,17 +47,19 @@
 
         remote = partial(grad_blk, chip ^ 1)
         from_sib = permute(half(remote, core ^ 1, rows), sib_perm)
-        chip_sum = half(remote, core, rows) + from_sib
-        arrived, start = [], 0
+        sums, arrived, start = [], [], 0
         for size in CHUNKS:
-            arrived.append(permute(chip_sum[start:start + size], peer_perm))
+            mine = lax.dynamic_slice_in_dim(remote, core * rows + start, size, 0, allow_negative_indices=False)
+            sums.append(mine + from_sib[start:start + size])
+            arrived.append(permute(sums[-1], peer_perm))
             start += size
 
-        grad_late, _ = lax.optimization_barrier((grad_blk, chip_sum))
+        grad_late, *_ = lax.optimization_barrier((grad_blk, *sums))
         local = partial(grad_late, chip)
         own = half(local, core, rows) + permute(half(local, core ^ 1, rows), sib_perm)
 
-        grad_w = weight_term(pair(x_blk, x_sib, core), grad_late, chip)
+        x_local = pair(x_blk, x_sib, core)
+        grad_w = weight_term(x_local, grad_late, chip)
         grad_w = grad_w + weight_term(pair(x_peer, x_opp, core), grad_late, chip ^ 1)
 
         grad_x, start = jnp.zeros(x_blk.shape, jnp.bfloat16), 0

time: 689 us -> 667 us (0.968)
  local copies, waits for them, and re-layouts: 52.3 us -> 33.4 us
  waiting for transfers between devices: 232 us -> 224 us
    slice x4 -> x0, local copies, waits for them, and re-layouts: 18.9 us -> none  [per_device(): arrived.append(permute(chip_sum[start:start + size], peer_perm))]
    ppermute x9, waiting for transfers between devices: 232 us -> 224 us  [permute(): return lax.ppermute(value, 'tp', perm)]
    add x1 -> x4, other arithmetic: 17.4 us -> 23.7 us  [per_device(): sums.append(mine + from_sib[start:start + size])]
where the time goes in v2:
time: 667 us; the launch traced here: 666 us
  matrix products  329 us (49%)
  waiting for transfers between devices  224 us (34%)
  other arithmetic  72.2 us (11%)
  local copies, waits for them, and re-layouts  33.4 us (5%)
  starting transfers between devices  7.59 us (1%)
    ppermute x9, waiting for transfers between devices, permute(): return lax.ppermute(value, 'tp', perm)  224 us
    dot_general x2, matrix products, weight_term(): lax.dot_general(x_rows, chip_rows(grad, which), (((0,), (0,)), ((), ())),...  171 us
    dot_general x2, matrix products, partial(): lax.dot_general(chip_rows(grad, which), w_blk, (((1,), (1,)), ((), ())),...  158 us
    add x4, other arithmetic, per_device(): sums.append(mine + from_sib[start:start + size])  23.7 us
    dynamic_slice x2, local copies, waits for them, and re-layouts, half(): lax.dynamic_slice_in_dim(value, core * rows, rows, 0, allow_negative_indi...  23.2 us
    select_n x2, other arithmetic, pair(): first = jnp.where(core == 0, mine, other)  22.8 us
  transfers between devices with their start and end apart: 9, of which 4 were waited for; matrix products, arithmetic and copies ran while one was open for 51% of the time, Pallas kernels for 0%

profile of v2, /device:TPU:0, one launch (start us, length us, event | category | flops | bytes accessed | tf_op | source)
XLA Modules:
  0.0 666.4 jit_solution(12168740619801851006)
XLA Ops:
  0.6 78.8 %fusion.2 = f32[4096,2048]{1,0:T(8,128)} fusion(bf16[2048,4096]{1,0:T(8,128)(2,1)} %param.4, bf16[8192,4096]{1,0:T(8,128)(2,1)} %param.5, s32[]{:T(128)S(6)} %mul.8), kind=kOutput, calls=%fused_computation.2 | convolution fusion | flops 68719476736 | bytes 83886080 | tf_op jit(solution)/shard_map/dot_general | solution.py:35
  79.5 11.6 %constant_dynamic-slice_fusion.1 = f32[2048,2048]{1,0:T(8,128)} fusion(f32[4096,2048]{1,0:T(8,128)} %fusion.2, s32[]{:T(128)S(6)} %mul.10), kind=kLoop, calls=%fused_computation.39 | loop fusion | bytes 33554436 | tf_op jit(solution)/shard_map/dynamic_slice | solution.py:19
  91.1 0.9 collective-permute-start
  92.0 2.4 collective-permute-start.7
  94.4 0.2 collective-permute-start.6
  94.6 181.2 %collective-permute-done.7 = bf16[2048,2048]{1,0:T(8,128)(2,1)} collective-permute-done((bf16[2048,2048]{1,0:T(8,128)(2,1)}, bf16[2048,2048]{1,0:T(8,128)(2,1)}, u32[]{:S(2)}, u32[]{:S(2)}) %collective-permute-start.7) | collective-permute-done | bytes 8388640 | tf_op jit(solution)/shard_map/ppermute | solution.py:16
  275.9 0.0 collective-permute-start.8
  275.9 0.0 collective-permute-done.6
  275.9 11.4 %broadcast_select_fusion.3 = (bf16[2048,2048]{1,0:T(8,128)(2,1)}, bf16[2048,2048]{1,0:T(8,128)(2,1)}) fusion(bf16[2048,2048]{1,0:T(8,128)(2,1)} %param.3, bf16[2048,2048]{1,0:T(8,128)(2,1)} %collective-permute-done.6, pred[]{:T(512)S(6)} %eq.2), kind=kLoop, calls=%fused_computation.22 | loop fusion | flops 8388608 | bytes 33554432 | tf_op jit(solution)/shard_map/jit(_where)/select_n | solution.py:22
  287.3 0.0 collective-permute-done
  287.3 14.4 %slice_add_fusion.1 = f32[1536,2048]{1,0:T(8,128)} fusion(f32[2048,2048]{1,0:T(8,128)} %collective-permute-done, f32[4096,2048]{1,0:T(8,128)} %fusion.2, s32[]{:T(128)S(6)} %mul.9), kind=kLoop, calls=%fused_computation.18 | loop fusion | flops 3145728 | bytes 37748740 | tf_op jit(solution)/shard_map/add | solution.py:53
  301.7 1.7 collective-permute-start.2
  303.5 5.2 slice_add_fusion.3
  308.6 0.3 collective-permute-start.3
  308.9 2.3 slice_add_fusion.5
  311.3 1.7 collective-permute-start.4
  313.0 1.8 slice_add_fusion.7
  314.8 0.3 collective-permute-start.5
  315.1 78.9 %fusion.6 = f32[4096,2048]{1,0:T(8,128)} fusion(bf16[2048,4096]{1,0:T(8,128)(2,1)} %param.4, bf16[8192,4096]{1,0:T(8,128)(2,1)} %param.5, s32[]{:T(128)S(6)} %mul.11), kind=kOutput, calls=%fused_computation.6 | convolution fusion | flops 68719476736 | bytes 83886080 | tf_op jit(solution)/shard_map/dot_general | solution.py:35
  393.9 11.6 %constant_dynamic-slice_fusion = f32[2048,2048]{1,0:T(8,128)} fusion(f32[4096,2048]{1,0:T(8,128)} %fusion.6, s32[]{:T(128)S(6)} %mul.10), kind=kLoop, calls=%fused_computation.37 | loop fusion | bytes 33554436 | tf_op jit(solution)/shard_map/dynamic_slice | solution.py:19
  405.6 80.6 %fusion.4 = f32[2048,4096]{1,0:T(8,128)} fusion(bf16[8192,4096]{1,0:T(8,128)(2,1)} %param.5, s32[]{:T(128)S(6)} %mul.11, bf16[2048,2048]{1,0:T(8,128)(2,1)} %get-tuple-element.7, bf16[2048,2048]{1,0:T(8,128)(2,1)} %get-tuple-element.6), kind=kOutput, calls=%fused_computation.4 | convolution fusion | flops 68753031168 | bytes 83886080 | tf_op jit(solution)/shard_map/dot_general | solution.py:40
  486.2 0.0 collective-permute-done.8
  486.2 0.0 collective-permute-start.1
  486.2 11.4 %broadcast_select_fusion.1 = (bf16[2048,2048]{1,0:T(8,128)(2,1)}, bf16[2048,2048]{1,0:T(8,128)(2,1)}) fusion(bf16[2048,2048]{1,0:T(8,128)(2,1)} %collective-permute-done.7, bf16[2048,2048]{1,0:T(8,128)(2,1)} %collective-permute-done.8, pred[]{:T(512)S(6)} %eq.2), kind=kLoop, calls=%fused_computation.20 | loop fusion | flops 8388608 | bytes 33554432 | tf_op jit(solution)/shard_map/jit(_where)/select_n | solution.py:22
  497.6 90.5 %fusion.8 = f32[2048,4096]{1,0:T(8,128)} fusion(f32[2048,4096]{1,0:T(8,128)} %fusion.4, bf16[8192,4096]{1,0:T(8,128)(2,1)} %param.5, s32[]{:T(128)S(6)} %mul.8, bf16[2048,2048]{1,0:T(8,128)(2,1)} %get-tuple-element.5, bf16[2048,2048]{1,0:T(8,128)(2,1)} %get-tuple-element.4), kind=kOutput, calls=%fused_computation.8 | convolution fusion | flops 68761419776 | bytes 117440512 | tf_op jit(solution)/shard_map/dot_general | solution.py:40
  588.1 0.0 collective-permute-done.1
  588.1 11.6 %dynamic-slice_add_fusion = f32[2048,2048]{1,0:T(8,128)S(1)} fusion(f32[2048,2048]{1,0:T(8,128)} %collective-permute-done.1, f32[4096,2048]{1,0:T(8,128)} %fusion.6, s32[]{:T(128)S(6)} %mul.9), kind=kLoop, calls=%fused_computation.15 | loop fusion | flops 4194304 | bytes 50331652 | tf_op jit(solution)/shard_map/add | solution.py:59
  599.7 0.0 copy-start
  599.7 0.0 collective-permute-done.2
  599.7 5.7 copy-done
  605.5 5.7 fusion.17
  611.2 4.5 dynamic_update_slice.12
  615.7 27.0 %collective-permute-done.3 = f32[384,2048]{1,0:T(8,128)} collective-permute-done((f32[384,2048]{1,0:T(8,128)}, f32[384,2048]{1,0:T(8,128)}, u32[]{:S(2)}, u32[]{:S(2)}) %collective-permute-start.3) | collective-permute-done | bytes 3145760 | tf_op jit(solution)/shard_map/ppermute | solution.py:16
  642.7 4.4 fusion.19
  647.1 12.4 %collective-permute-done.4 = f32[96,2048]{1,0:T(8,128)} collective-permute-done((f32[96,2048]{1,0:T(8,128)}, f32[96,2048]{1,0:T(8,128)}, u32[]{:S(2)}, u32[]{:S(2)}) %collective-permute-start.4) | collective-permute-done | bytes 786464 | tf_op jit(solution)/shard_map/ppermute | solution.py:16
  659.5 2.2 fusion.21
  661.7 3.0 collective-permute-done.5
  664.7 1.7 fusion.23
Async XLA Ops:
  91.1 196.2 %collective-permute-start = (f32[2048,2048]{1,0:T(8,128)}, f32[2048,2048]{1,0:T(8,128)}, u32[]{:S(2)}, u32[]{:S(2)}) collective-permute-start(f32[2048,2048]{1,0:T(8,128)} %constant_dynamic-slice_fusion.1), channel_id=1, source_target_pairs={{0,1},{1,0},{2,3},{3,2},{4,5},{5,4},{6,7},{7,6}} | collective-permute-start | bytes 50331656 | tf_op jit(solution)/shard_map/ppermute | solution.py:16
  92.0 183.8 %collective-permute-start.7 = (bf16[2048,2048]{1,0:T(8,128)(2,1)}, bf16[2048,2048]{1,0:T(8,128)(2,1)}, u32[]{:S(2)}, u32[]{:S(2)}) collective-permute-start(bf16[2048,2048]{1,0:T(8,128)(2,1)} %param.3), channel_id=1, source_target_pairs={{0,2},{1,3},{2,0},{3,1},{4,6},{5,7},{6,4},{7,5}} | collective-permute-start | bytes 25165832 | tf_op jit(solution)/shard_map/ppermute | solution.py:16
  94.4 181.4 %collective-permute-start.6 = (bf16[2048,2048]{1,0:T(8,128)(2,1)}, bf16[2048,2048]{1,0:T(8,128)(2,1)}, u32[]{:S(2)}, u32[]{:S(2)}) collective-permute-start(bf16[2048,2048]{1,0:T(8,128)(2,1)} %param.3), channel_id=1, source_target_pairs={{0,1},{1,0},{2,3},{3,2},{4,5},{5,4},{6,7},{7,6}} | collective-permute-start | bytes 25165832 | tf_op jit(solution)/shard_map/ppermute | solution.py:16
  275.9 210.3 %collective-permute-start.8 = (bf16[2048,2048]{1,0:T(8,128)(2,1)}, bf16[2048,2048]{1,0:T(8,128)(2,1)}, u32[]{:S(2)}, u32[]{:S(2)}) collective-permute-start(bf16[2048,2048]{1,0:T(8,128)(2,1)} %collective-permute-done.7), channel_id=1, source_target_pairs={{0,1},{1,0},{2,3},{3,2},{4,5},{5,4},{6,7},{7,6}} | collective-permute-start | bytes 25165832 | tf_op jit(solution)/shard_map/ppermute | solution.py:16
  301.7 298.0 %collective-permute-start.2 = (f32[1536,2048]{1,0:T(8,128)}, f32[1536,2048]{1,0:T(8,128)}, u32[]{:S(2)}, u32[]{:S(2)}) collective-permute-start(f32[1536,2048]{1,0:T(8,128)} %slice_add_fusion.1), channel_id=1, source_target_pairs={{0,2},{1,3},{2,0},{3,1},{4,6},{5,7},{6,4},{7,5}} | collective-permute-start | bytes 37748744 | tf_op jit(solution)/shard_map/ppermute | solution.py:16
  308.6 334.0 %collective-permute-start.3 = (f32[384,2048]{1,0:T(8,128)}, f32[384,2048]{1,0:T(8,128)}, u32[]{:S(2)}, u32[]{:S(2)}) collective-permute-start(f32[384,2048]{1,0:T(8,128)} %slice_add_fusion.3), channel_id=1, source_target_pairs={{0,2},{1,3},{2,0},{3,1},{4,6},{5,7},{6,4},{7,5}} | collective-permute-start | bytes 9437192 | tf_op jit(solution)/shard_map/ppermute | solution.py:16
  311.3 348.2 %collective-permute-start.4 = (f32[96,2048]{1,0:T(8,128)}, f32[96,2048]{1,0:T(8,128)}, u32[]{:S(2)}, u32[]{:S(2)}) collective-permute-start(f32[96,2048]{1,0:T(8,128)} %slice_add_fusion.5), channel_id=1, source_target_pairs={{0,2},{1,3},{2,0},{3,1},{4,6},{5,7},{6,4},{7,5}} | collective-permute-start | bytes 2359304 | tf_op jit(solution)/shard_map/ppermute | solution.py:16
  314.8 349.9 %collective-permute-start.5 = (f32[32,2048]{1,0:T(8,128)}, f32[32,2048]{1,0:T(8,128)}, u32[]{:S(2)}, u32[]{:S(2)}) collective-permute-start(f32[32,2048]{1,0:T(8,128)} %slice_add_fusion.7), channel_id=1, source_target_pairs={{0,2},{1,3},{2,0},{3,1},{4,6},{5,7},{6,4},{7,5}} | collective-permute-start | bytes 786440 | tf_op jit(solution)/shard_map/ppermute | solution.py:16
  486.2 101.9 %collective-permute-start.1 = (f32[2048,2048]{1,0:T(8,128)}, f32[2048,2048]{1,0:T(8,128)}, u32[]{:S(2)}, u32[]{:S(2)}) collective-permute-start(f32[2048,2048]{1,0:T(8,128)} %constant_dynamic-slice_fusion), channel_id=1, source_target_pairs={{0,1},{1,0},{2,3},{3,2},{4,5},{5,4},{6,7},{7,6}} | collective-permute-start | bytes 50331656 | tf_op jit(solution)/shard_map/ppermute | solution.py:16
  599.7 5.7 copy-start

commit v3 on v2

--- a/solution.py
+++ b/solution.py
@@ -4,13 +4,15 @@
 from jax.sharding import PartitionSpec as P
 
 
-CHUNKS = (1536, 384, 96, 32)
+CHUNKS = (1536, 384, 80, 32)
+EXTRA = 16
 
 
 def solution(mesh):
     tp_size = mesh.shape["tp"]
     sib_perm = [(t, t ^ 1) for t in range(tp_size)]
     peer_perm = [(t, t ^ 2) for t in range(tp_size)]
+    core1 = [t for t in range(tp_size) if t % 2 == 1]
 
     def permute(value, perm):
         return lax.ppermute(value, "tp", perm)
@@ -54,6 +56,11 @@
             arrived.append(permute(sums[-1], peer_perm))
             start += size
 
+        last = remote[rows - EXTRA:rows]
+        last = last + permute(last, [(t ^ 1, t) for t in core1])
+        mine = remote[2 * rows - EXTRA:] + from_sib[rows - EXTRA:]
+        last = permute(jnp.concatenate((last, mine)), [(t, t ^ 2) for t in core1])
+
         grad_late, *_ = lax.optimization_barrier((grad_blk, *sums))
         local = partial(grad_late, chip)
         own = half(local, core, rows) + permute(half(local, core ^ 1, rows), sib_perm)
@@ -62,11 +69,13 @@
         grad_w = weight_term(x_local, grad_late, chip)
         grad_w = grad_w + weight_term(pair(x_peer, x_opp, core), grad_late, chip ^ 1)
 
-        grad_x, start = jnp.zeros(x_blk.shape, jnp.bfloat16), 0
-        for size, part in zip(CHUNKS, arrived):
+        to_core0 = permute(last[:EXTRA], [(t, t ^ 1) for t in core1])
+        arrived.insert(0, jnp.where(core == 0, to_core0, last[EXTRA:]))
+        grad_x, start = jnp.zeros(x_blk.shape, jnp.bfloat16), rows - EXTRA
+        for size, part in zip((EXTRA,) + CHUNKS, arrived):
             done = (own[start:start + size] + part).astype(jnp.bfloat16)
             grad_x = lax.dynamic_update_slice_in_dim(grad_x, done, start, 0)
-            start += size
+            start = (start + size) % rows
         return grad_x, grad_w
 
     return jax.shard_map(

time: 667 us -> 666 us (level)
  waiting for transfers between devices: 224 us -> 206 us
  other arithmetic: 72.2 us -> 80.7 us
  starting transfers between devices: 7.59 us -> 14.3 us
    ppermute x9 -> x12, waiting for transfers between devices: 224 us -> 206 us  [permute(): return lax.ppermute(value, 'tp', perm)]
    dynamic_update_slice x3 -> x4, other arithmetic: 8.32 us -> 20 us  [per_device(): grad_x = lax.dynamic_update_slice_in_dim(grad_x, done, start, 0)]
    ppermute x9 -> x12, starting transfers between devices: 7.59 us -> 14.3 us  [permute(): return lax.ppermute(value, 'tp', perm)]
  transfers between devices with their start and end apart: 9 -> 12, of which waited for: 4 -> 4; matrix products, arithmetic and copies ran while one was open for 51% -> 52% of each run, Pallas kernels for 0% -> 0%
where the time goes in v3:
time: 666 us
  matrix products  329 us (49%)
  waiting for transfers between devices  206 us (31%)
  other arithmetic  80.7 us (12%)
  local copies, waits for them, and re-layouts  35.3 us (5%)
  starting transfers between devices  14.3 us (2%)
    ppermute x12, waiting for transfers between devices, permute(): return lax.ppermute(value, 'tp', perm)  206 us
    dot_general x2, matrix products, weight_term(): lax.dot_general(x_rows, chip_rows(grad, which), (((0,), (0,)), ((), ())),...  171 us
    dot_general x2, matrix products, partial(): lax.dot_general(chip_rows(grad, which), w_blk, (((1,), (1,)), ((), ())),...  158 us
    add x4, other arithmetic, per_device(): sums.append(mine + from_sib[start:start + size])  23.5 us
    dynamic_slice x2, local copies, waits for them, and re-layouts, half(): lax.dynamic_slice_in_dim(value, core * rows, rows, 0, allow_negative_indi...  23.3 us
    select_n x2, other arithmetic, pair(): first = jnp.where(core == 0, mine, other)  22.9 us
    dynamic_update_slice x4, other arithmetic, per_device(): grad_x = lax.dynamic_update_slice_in_dim(grad_x, done, start, 0)  20 us
    ppermute x12, starting transfers between devices, permute(): return lax.ppermute(value, 'tp', perm)  14.3 us
  transfers between devices with their start and end apart: 12, of which 4 were waited for; matrix products, arithmetic and copies ran while one was open for 52% of the time, Pallas kernels for 0%

profile of v3, /device:TPU:0, one launch (start us, length us, event | category | flops | bytes accessed | tf_op | source)
XLA Modules:
  0.0 666.0 jit_solution(8412153870503610692)
XLA Ops:
  0.6 78.8 %fusion.2 = f32[4096,2048]{1,0:T(8,128)} fusion(bf16[2048,4096]{1,0:T(8,128)(2,1)} %param.4, bf16[8192,4096]{1,0:T(8,128)(2,1)} %param.5, s32[]{:T(128)S(6)} %mul.8), kind=kOutput, calls=%fused_computation.2 | convolution fusion | flops 68719476736 | bytes 83886080 | tf_op jit(solution)/shard_map/dot_general | solution.py:37
  79.5 11.6 %constant_dynamic-slice_fusion.1 = f32[2048,2048]{1,0:T(8,128)} fusion(f32[4096,2048]{1,0:T(8,128)} %fusion.2, s32[]{:T(128)S(6)} %mul.10), kind=kLoop, calls=%fused_computation.45 | loop fusion | bytes 33554436 | tf_op jit(solution)/shard_map/dynamic_slice | solution.py:21
  91.1 0.9 collective-permute-start
  92.0 2.4 collective-permute-start.10
  94.4 0.2 collective-permute-start.9
  94.7 0.9 slice.61
  95.6 2.2 collective-permute-start.2
  97.8 178.1 %collective-permute-done.10 = bf16[2048,2048]{1,0:T(8,128)(2,1)} collective-permute-done((bf16[2048,2048]{1,0:T(8,128)(2,1)}, bf16[2048,2048]{1,0:T(8,128)(2,1)}, u32[]{:S(2)}, u32[]{:S(2)}) %collective-permute-start.10) | collective-permute-done | bytes 8388640 | tf_op jit(solution)/shard_map/ppermute | solution.py:18
  275.9 0.0 collective-permute-start.11
  275.9 0.0 collective-permute-done.9
  275.9 11.5 %broadcast_select_fusion.3 = (bf16[2048,2048]{1,0:T(8,128)(2,1)}, bf16[2048,2048]{1,0:T(8,128)(2,1)}) fusion(bf16[2048,2048]{1,0:T(8,128)(2,1)} %param.3, bf16[2048,2048]{1,0:T(8,128)(2,1)} %collective-permute-done.9, pred[]{:T(512)S(6)} %eq.2), kind=kLoop, calls=%fused_computation.22 | loop fusion | flops 8388608 | bytes 33554432 | tf_op jit(solution)/shard_map/jit(_where)/select_n | solution.py:24
  287.3 0.0 collective-permute-done.2
  287.3 0.0 collective-permute-done
  287.3 1.1 slice_add_fusion.9
  288.4 0.7 pad_maximum_fusion
  289.1 1.4 collective-permute-start.3
  290.5 14.4 %slice_add_fusion.1 = f32[1536,2048]{1,0:T(8,128)} fusion(f32[2048,2048]{1,0:T(8,128)} %collective-permute-done, f32[4096,2048]{1,0:T(8,128)} %fusion.2, s32[]{:T(128)S(6)} %mul.9), kind=kLoop, calls=%fused_computation.18 | loop fusion | flops 3145728 | bytes 37748740 | tf_op jit(solution)/shard_map/add | solution.py:55
  304.9 1.7 collective-permute-start.5
  306.6 5.2 slice_add_fusion.3
  311.8 0.3 collective-permute-start.6
  312.1 2.2 slice_add_fusion.5
  314.3 1.7 collective-permute-start.7
  316.0 1.7 slice_add_fusion.7
  317.8 79.0 %fusion.6 = f32[4096,2048]{1,0:T(8,128)} fusion(bf16[2048,4096]{1,0:T(8,128)(2,1)} %param.4, bf16[8192,4096]{1,0:T(8,128)(2,1)} %param.5, s32[]{:T(128)S(6)} %mul.11), kind=kOutput, calls=%fused_computation.6 | convolution fusion | flops 68719476736 | bytes 83886080 | tf_op jit(solution)/shard_map/dot_general | solution.py:37
  396.7 11.6 %constant_dynamic-slice_fusion = f32[2048,2048]{1,0:T(8,128)} fusion(f32[4096,2048]{1,0:T(8,128)} %fusion.6, s32[]{:T(128)S(6)} %mul.10), kind=kLoop, calls=%fused_computation.43 | loop fusion | bytes 33554436 | tf_op jit(solution)/shard_map/dynamic_slice | solution.py:21
  408.4 80.6 %fusion.4 = f32[2048,4096]{1,0:T(8,128)} fusion(bf16[8192,4096]{1,0:T(8,128)(2,1)} %param.5, s32[]{:T(128)S(6)} %mul.11, bf16[2048,2048]{1,0:T(8,128)(2,1)} %get-tuple-element.9, bf16[2048,2048]{1,0:T(8,128)(2,1)} %get-tuple-element.8), kind=kOutput, calls=%fused_computation.4 | convolution fusion | flops 68753031168 | bytes 83886080 | tf_op jit(solution)/shard_map/dot_general | solution.py:42
  489.0 0.0 collective-permute-done.11
  489.0 0.4 collective-permute-start.1
  489.4 11.4 %broadcast_select_fusion.1 = (bf16[2048,2048]{1,0:T(8,128)(2,1)}, bf16[2048,2048]{1,0:T(8,128)(2,1)}) fusion(bf16[2048,2048]{1,0:T(8,128)(2,1)} %collective-permute-done.10, bf16[2048,2048]{1,0:T(8,128)(2,1)} %collective-permute-done.11, pred[]{:T(512)S(6)} %eq.2), kind=kLoop, calls=%fused_computation.20 | loop fusion | flops 8388608 | bytes 33554432 | tf_op jit(solution)/shard_map/jit(_where)/select_n | solution.py:24
  500.8 90.5 %fusion.8 = f32[2048,4096]{1,0:T(8,128)} fusion(f32[2048,4096]{1,0:T(8,128)} %fusion.4, bf16[8192,4096]{1,0:T(8,128)(2,1)} %param.5, s32[]{:T(128)S(6)} %mul.8, bf16[2048,2048]{1,0:T(8,128)(2,1)} %get-tuple-element.7, bf16[2048,2048]{1,0:T(8,128)(2,1)} %get-tuple-element.6), kind=kOutput, calls=%fused_computation.8 | convolution fusion | flops 68761419776 | bytes 117440512 | tf_op jit(solution)/shard_map/dot_general | solution.py:42
  591.3 0.0 collective-permute-done.3
  591.3 1.7 collective-permute-start.8
  593.0 0.9 slice.64
  593.9 0.0 collective-permute-done.1
  593.9 1.3 collective-permute-start.4
  595.2 11.6 %dynamic-slice_add_fusion = f32[2048,2048]{1,0:T(8,128)S(1)} fusion(f32[2048,2048]{1,0:T(8,128)} %collective-permute-done.1, f32[4096,2048]{1,0:T(8,128)} %fusion.6, s32[]{:T(128)S(6)} %mul.9), kind=kLoop, calls=%fused_computation.15 | loop fusion | flops 4194304 | bytes 50331652 | tf_op jit(solution)/shard_map/add | solution.py:66
  606.9 0.0 collective-permute-done.4
  606.9 5.7 copy-done
  612.6 0.9 fusion.26
  613.6 4.5 dynamic_update_slice.15
  618.0 0.0 collective-permute-done.5
  618.0 11.8 %fusion.18 = bf16[2048,2048]{1,0:T(8,128)(2,1)} fusion(bf16[2048,2048]{1,0:T(8,128)(2,1)} %dynamic_update_slice.15, f32[1536,2048]{1,0:T(8,128)} %collective-permute-done.5, f32[2048,2048]{1,0:T(8,128)} %copy-done), kind=kLoop, calls=%fused_computation.23 | loop fusion | flops 6291456 | bytes 31457280 | tf_op jit(solution)/shard_map/dynamic_update_slice | solution.py:77
  629.9 14.9 %collective-permute-done.6 = f32[384,2048]{1,0:T(8,128)} collective-permute-done((f32[384,2048]{1,0:T(8,128)}, f32[384,2048]{1,0:T(8,128)}, u32[]{:S(2)}, u32[]{:S(2)}) %collective-permute-start.6) | collective-permute-done | bytes 3145760 | tf_op jit(solution)/shard_map/ppermute | solution.py:18
  644.8 4.4 fusion.20
  649.2 9.6 %collective-permute-done.7 = f32[80,2048]{1,0:T(8,128)} collective-permute-done((f32[80,2048]{1,0:T(8,128)}, f32[80,2048]{1,0:T(8,128)}, u32[]{:S(2)}, u32[]{:S(2)}) %collective-permute-start.7) | collective-permute-done | bytes 655392 | tf_op jit(solution)/shard_map/ppermute | solution.py:18
  658.9 2.1 fusion.22
  660.9 3.4 collective-permute-done.8
  664.4 1.7 fusion.24
  (3 shorter events, 0.0 us)
Async XLA Ops:
  91.1 196.2 %collective-permute-start = (f32[2048,2048]{1,0:T(8,128)}, f32[2048,2048]{1,0:T(8,128)}, u32[]{:S(2)}, u32[]{:S(2)}) collective-permute-start(f32[2048,2048]{1,0:T(8,128)} %constant_dynamic-slice_fusion.1), channel_id=1, source_target_pairs={{0,1},{1,0},{2,3},{3,2},{4,5},{5,4},{6,7},{7,6}} | collective-permute-start | bytes 50331656 | tf_op jit(solution)/shard_map/ppermute | solution.py:18
  92.0 183.8 %collective-permute-start.10 = (bf16[2048,2048]{1,0:T(8,128)(2,1)}, bf16[2048,2048]{1,0:T(8,128)(2,1)}, u32[]{:S(2)}, u32[]{:S(2)}) collective-permute-start(bf16[2048,2048]{1,0:T(8,128)(2,1)} %param.3), channel_id=1, source_target_pairs={{0,2},{1,3},{2,0},{3,1},{4,6},{5,7},{6,4},{7,5}} | collective-permute-start | bytes 25165832 | tf_op jit(solution)/shard_map/ppermute | solution.py:18
  94.4 181.4 %collective-permute-start.9 = (bf16[2048,2048]{1,0:T(8,128)(2,1)}, bf16[2048,2048]{1,0:T(8,128)(2,1)}, u32[]{:S(2)}, u32[]{:S(2)}) collective-permute-start(bf16[2048,2048]{1,0:T(8,128)(2,1)} %param.3), channel_id=1, source_target_pairs={{0,1},{1,0},{2,3},{3,2},{4,5},{5,4},{6,7},{7,6}} | collective-permute-start | bytes 25165832 | tf_op jit(solution)/shard_map/ppermute | solution.py:18
  95.6 191.8 %collective-permute-start.2 = (f32[16,2048]{1,0:T(8,128)S(1)}, f32[16,2048]{1,0:T(8,128)S(1)}, u32[]{:S(2)}, u32[]{:S(2)}) collective-permute-start(f32[16,2048]{1,0:T(8,128)S(1)} %slice.61), channel_id=1, source_target_pairs={{0,1},{2,3},{4,5},{6,7}} | collective-permute-start | bytes 393224 | tf_op jit(solution)/shard_map/ppermute | solution.py:18
  275.9 213.1 %collective-permute-start.11 = (bf16[2048,2048]{1,0:T(8,128)(2,1)}, bf16[2048,2048]{1,0:T(8,128)(2,1)}, u32[]{:S(2)}, u32[]{:S(2)}) collective-permute-start(bf16[2048,2048]{1,0:T(8,128)(2,1)} %collective-permute-done.10), channel_id=1, source_target_pairs={{0,1},{1,0},{2,3},{3,2},{4,5},{5,4},{6,7},{7,6}} | collective-permute-start | bytes 25165832 | tf_op jit(solution)/shard_map/ppermute | solution.py:18
  289.1 302.1 %collective-permute-start.3 = (f32[32,2048]{1,0:T(8,128)}, f32[32,2048]{1,0:T(8,128)}, u32[]{:S(2)}, u32[]{:S(2)}) collective-permute-start(f32[32,2048]{1,0:T(8,128)} %pad_maximum_fusion), channel_id=1, source_target_pairs={{1,3},{3,1},{5,7},{7,5}} | collective-permute-start | bytes 786440 | tf_op jit(solution)/shard_map/ppermute | solution.py:18
  304.9 313.2 %collective-permute-start.5 = (f32[1536,2048]{1,0:T(8,128)}, f32[1536,2048]{1,0:T(8,128)}, u32[]{:S(2)}, u32[]{:S(2)}) collective-permute-start(f32[1536,2048]{1,0:T(8,128)} %slice_add_fusion.1), channel_id=1, source_target_pairs={{0,2},{1,3},{2,0},{3,1},{4,6},{5,7},{6,4},{7,5}} | collective-permute-start | bytes 37748744 | tf_op jit(solution)/shard_map/ppermute | solution.py:18
  311.8 333.0 %collective-permute-start.6 = (f32[384,2048]{1,0:T(8,128)}, f32[384,2048]{1,0:T(8,128)}, u32[]{:S(2)}, u32[]{:S(2)}) collective-permute-start(f32[384,2048]{1,0:T(8,128)} %slice_add_fusion.3), channel_id=1, source_target_pairs={{0,2},{1,3},{2,0},{3,1},{4,6},{5,7},{6,4},{7,5}} | collective-permute-start | bytes 9437192 | tf_op jit(solution)/shard_map/ppermute | solution.py:18
  314.3 344.6 %collective-permute-start.7 = (f32[80,2048]{1,0:T(8,128)}, f32[80,2048]{1,0:T(8,128)}, u32[]{:S(2)}, u32[]{:S(2)}) collective-permute-start(f32[80,2048]{1,0:T(8,128)} %slice_add_fusion.5), channel_id=1, source_target_pairs={{0,2},{1,3},{2,0},{3,1},{4,6},{5,7},{6,4},{7,5}} | collective-permute-start | bytes 1966088 | tf_op jit(solution)/shard_map/ppermute | solution.py:18
  489.0 105.0 %collective-permute-start.1 = (f32[2048,2048]{1,0:T(8,128)}, f32[2048,2048]{1,0:T(8,128)}, u32[]{:S(2)}, u32[]{:S(2)}) collective-permute-start(f32[2048,2048]{1,0:T(8,128)} %constant_dynamic-slice_fusion), channel_id=1, source_target_pairs={{0,1},{1,0},{2,3},{3,2},{4,5},{5,4},{6,7},{7,6}} | collective-permute-start | bytes 50331656 | tf_op jit(solution)/shard_map/ppermute | solution.py:18
  500.8 90.5 %copy-start.1 = (f32[32,2048]{1,0:T(8,128)S(1)}, f32[32,2048]{1,0:T(8,128)}, u32[]{:S(2)}) copy-start(f32[32,2048]{1,0:T(8,128)} %slice_add_fusion.7) | copy-start | bytes 786436
  591.3 73.1 %collective-permute-start.8 = (f32[32,2048]{1,0:T(8,128)S(1)}, f32[32,2048]{1,0:T(8,128)S(1)}, u32[]{:S(2)}, u32[]{:S(2)}) collective-permute-start(f32[32,2048]{1,0:T(8,128)S(1)} %copy-done.1), channel_id=1, source_target_pairs={{0,2},{1,3},{2,0},{3,1},{4,6},{5,7},{6,4},{7,5}} | collective-permute-start | bytes 786440 | tf_op jit(solution)/shard_map/ppermute | solution.py:18
  593.9 13.0 %collective-permute-start.4 = (f32[16,2048]{1,0:T(8,128)S(1)}, f32[16,2048]{1,0:T(8,128)S(1)}, u32[]{:S(2)}, u32[]{:S(2)}) collective-permute-start(f32[16,2048]{1,0:T(8,128)S(1)} %slice.64), channel_id=1, source_target_pairs={{1,0},{3,2},{5,4},{7,6}} | collective-permute-start | bytes 393224 | tf_op jit(solution)/shard_map/ppermute | solution.py:18
  606.9 5.7 copy-start

commit v4 on v3

--- a/solution.py
+++ b/solution.py
@@ -1,11 +1,34 @@
 import jax
 import jax.numpy as jnp
 from jax import lax
+from jax.experimental import pallas as pl
+from jax.experimental.pallas import tpu as pltpu
 from jax.sharding import PartitionSpec as P
 
 
-CHUNKS = (1536, 384, 80, 32)
+CHUNKS = (1600, 368, 64)
 EXTRA = 16
+
+
+def add_rows(start, part, own, grad_x):
+    size = part.shape[0]
+
+    def kernel(part_ref, own_ref, _, out_ref, total, sem):
+        total[...] = (own_ref[...] + part_ref[...]).astype(total.dtype)
+        copy = pltpu.make_async_copy(total, out_ref.at[pl.ds(start, size)], sem)
+        copy.start()
+        copy.wait()
+
+    return pl.pallas_call(
+        kernel,
+        out_shape=jax.ShapeDtypeStruct(grad_x.shape, grad_x.dtype),
+        in_specs=[pl.BlockSpec(memory_space=pltpu.VMEM)] * 2 + [pl.BlockSpec(memory_space=pl.ANY)],
+        out_specs=pl.BlockSpec(memory_space=pl.ANY),
+        scratch_shapes=[pltpu.VMEM(part.shape, grad_x.dtype), pltpu.SemaphoreType.DMA],
+        input_output_aliases={2: 0},
+        cost_estimate=pl.CostEstimate(flops=part.size, bytes_accessed=10 * part.size, transcendentals=0),
+        name="add_rows",
+    )(pltpu.with_memory_space_constraint(part, pltpu.VMEM), pltpu.with_memory_space_constraint(own, pltpu.VMEM), grad_x)
 
 
 def solution(mesh):
@@ -50,10 +73,11 @@
         remote = partial(grad_blk, chip ^ 1)
         from_sib = permute(half(remote, core ^ 1, rows), sib_perm)
         sums, arrived, start = [], [], 0
-        for size in CHUNKS:
+        for i, size in enumerate(CHUNKS):
             mine = lax.dynamic_slice_in_dim(remote, core * rows + start, size, 0, allow_negative_indices=False)
             sums.append(mine + from_sib[start:start + size])
-            arrived.append(permute(sums[-1], peer_perm))
+            if i < len(CHUNKS) - 1:
+                arrived.append(permute(sums[-1], peer_perm))
             start += size
 
         last = remote[rows - EXTRA:rows]
@@ -61,7 +85,7 @@
         mine = remote[2 * rows - EXTRA:] + from_sib[rows - EXTRA:]
         last = permute(jnp.concatenate((last, mine)), [(t, t ^ 2) for t in core1])
 
-        grad_late, *_ = lax.optimization_barrier((grad_blk, *sums))
+        grad_late, *_ = lax.optimization_barrier((grad_blk, *sums[:-1]))
         local = partial(grad_late, chip)
         own = half(local, core, rows) + permute(half(local, core ^ 1, rows), sib_perm)
 
@@ -69,10 +93,15 @@
         grad_w = weight_term(x_local, grad_late, chip)
         grad_w = grad_w + weight_term(pair(x_peer, x_opp, core), grad_late, chip ^ 1)
 
+        final, grad_w = lax.optimization_barrier((sums[-1], grad_w))
+        arrived.append(permute(final, peer_perm))
         to_core0 = permute(last[:EXTRA], [(t, t ^ 1) for t in core1])
         arrived.insert(0, jnp.where(core == 0, to_core0, last[EXTRA:]))
         grad_x, start = jnp.zeros(x_blk.shape, jnp.bfloat16), rows - EXTRA
         for size, part in zip((EXTRA,) + CHUNKS, arrived):
+            if part is arrived[-1]:
+                grad_x = add_rows(start, part, own[start:start + size], grad_x)
+                break
             done = (own[start:start + size] + part).astype(jnp.bfloat16)
             grad_x = lax.dynamic_update_slice_in_dim(grad_x, done, start, 0)
             start = (start + size) % rows

time: 666 us -> 688 us (1.033)
  the two profiles are of different devices: /device:TPU:0 before, /device:TPU:1 now
where the time goes in v4:
time: 688 us
  matrix products  329 us (48%)
  waiting for transfers between devices  236 us (34%)
  other arithmetic  74.9 us (11%)
  local copies, waits for them, and re-layouts  35.4 us (5%)
  starting transfers between devices  11.1 us (2%)
    ppermute x11, waiting for transfers between devices, permute(): return lax.ppermute(value, 'tp', perm)  236 us
    dot_general x2, matrix products, weight_term(): lax.dot_general(x_rows, chip_rows(grad, which), (((0,), (0,)), ((), ())),...  171 us
    dot_general x2, matrix products, partial(): lax.dot_general(chip_rows(grad, which), w_blk, (((1,), (1,)), ((), ())),...  158 us
    dynamic_slice x2, local copies, waits for them, and re-layouts, half(): lax.dynamic_slice_in_dim(value, core * rows, rows, 0, allow_negative_indi...  23.4 us
    select_n x2, other arithmetic, pair(): first = jnp.where(core == 0, mine, other)  22.8 us
    add x3, other arithmetic, per_device(): sums.append(mine + from_sib[start:start + size])  21.3 us
    dynamic_update_slice x2, other arithmetic, per_device(): grad_x = lax.dynamic_update_slice_in_dim(grad_x, done, start, 0)  16.3 us
  transfers between devices with their start and end apart: 11, of which 2 were waited for; matrix products, arithmetic and copies ran while one was open for 50% of the time, Pallas kernels for 0%

profile of v4, /device:TPU:1, one launch (start us, length us, event | category | flops | bytes accessed | tf_op | source)
XLA Modules:
  0.0 688.2 jit_solution(18407850541739410714)
XLA Ops:
  0.6 79.0 %fusion.2 = f32[4096,2048]{1,0:T(8,128)} fusion(bf16[2048,4096]{1,0:T(8,128)(2,1)} %param.4, bf16[8192,4096]{1,0:T(8,128)(2,1)} %param.5, s32[]{:T(128)S(6)} %mul.8), kind=kOutput, calls=%fused_computation.2 | convolution fusion | flops 68719476736 | bytes 83886080 | tf_op jit(solution)/shard_map/dot_general | solution.py:60
  79.6 11.8 %constant_dynamic-slice_fusion.1 = f32[2048,2048]{1,0:T(8,128)} fusion(f32[4096,2048]{1,0:T(8,128)} %fusion.2, s32[]{:T(128)S(6)} %mul.10), kind=kLoop, calls=%fused_computation.38 | loop fusion | bytes 33554436 | tf_op jit(solution)/shard_map/dynamic_slice | solution.py:44
  91.4 0.0 collective-permute-start
  91.4 2.6 collective-permute-start.2
  94.0 0.3 collective-permute-start.1
  94.3 0.9 slice.53
  95.2 1.3 collective-permute-start.6
  96.5 178.6 %collective-permute-done.2 = bf16[2048,2048]{1,0:T(8,128)(2,1)} collective-permute-done((bf16[2048,2048]{1,0:T(8,128)(2,1)}, bf16[2048,2048]{1,0:T(8,128)(2,1)}, u32[]{:S(2)}, u32[]{:S(2)}) %collective-permute-start.2) | collective-permute-done | bytes 8388640 | tf_op jit(solution)/shard_map/ppermute | solution.py:41
  275.2 0.6 collective-permute-start.3
  275.8 0.0 collective-permute-done.1
  275.8 11.4 %broadcast_select_fusion.3 = (bf16[2048,2048]{1,0:T(8,128)(2,1)}, bf16[2048,2048]{1,0:T(8,128)(2,1)}) fusion(bf16[2048,2048]{1,0:T(8,128)(2,1)} %param.3, bf16[2048,2048]{1,0:T(8,128)(2,1)} %collective-permute-done.1, pred[]{:T(512)S(6)} %eq.2), kind=kLoop, calls=%fused_computation.22 | loop fusion | flops 8388608 | bytes 33554432 | tf_op jit(solution)/shard_map/jit(_where)/select_n | solution.py:47
  287.2 0.0 collective-permute-done
  287.2 5.1 slice_add_fusion.3
  292.3 1.5 collective-permute-start.10
  293.8 15.0 %slice_add_fusion.1 = f32[1600,2048]{1,0:T(8,128)} fusion(f32[2048,2048]{1,0:T(8,128)} %collective-permute-done, f32[4096,2048]{1,0:T(8,128)} %fusion.2, s32[]{:T(128)S(6)} %mul.9), kind=kLoop, calls=%fused_computation.18 | loop fusion | flops 3276800 | bytes 39321604 | tf_op jit(solution)/shard_map/add | solution.py:78
  308.7 0.0 collective-permute-start.9
  308.7 0.0 collective-permute-done.6
  308.7 1.1 slice_add_fusion.6
  309.8 0.7 pad_maximum_fusion
  310.5 3.5 collective-permute-start.7
  314.1 79.0 %fusion.4 = f32[4096,2048]{1,0:T(8,128)} fusion(bf16[2048,4096]{1,0:T(8,128)(2,1)} %param.4, bf16[8192,4096]{1,0:T(8,128)(2,1)} %param.5, s32[]{:T(128)S(6)} %mul.11), kind=kOutput, calls=%fused_computation.4 | convolution fusion | flops 68719476736 | bytes 83886080 | tf_op jit(solution)/shard_map/dot_general | solution.py:60
  393.0 11.6 %constant_dynamic-slice_fusion = f32[2048,2048]{1,0:T(8,128)} fusion(f32[4096,2048]{1,0:T(8,128)} %fusion.4, s32[]{:T(128)S(6)} %mul.10), kind=kLoop, calls=%fused_computation.35 | loop fusion | bytes 33554436 | tf_op jit(solution)/shard_map/dynamic_slice | solution.py:44
  404.7 0.0 collective-permute-start.5
  404.7 80.9 %fusion.6 = f32[2048,4096]{1,0:T(8,128)} fusion(bf16[8192,4096]{1,0:T(8,128)(2,1)} %param.5, s32[]{:T(128)S(6)} %mul.11, bf16[2048,2048]{1,0:T(8,128)(2,1)} %get-tuple-element.13, bf16[2048,2048]{1,0:T(8,128)(2,1)} %get-tuple-element.12), kind=kOutput, calls=%fused_computation.6 | convolution fusion | flops 68753031168 | bytes 83886080 | tf_op jit(solution)/shard_map/dot_general | solution.py:65
  485.5 0.0 collective-permute-done.3
  485.5 11.4 %broadcast_select_fusion.1 = (bf16[2048,2048]{1,0:T(8,128)(2,1)}, bf16[2048,2048]{1,0:T(8,128)(2,1)}) fusion(bf16[2048,2048]{1,0:T(8,128)(2,1)} %collective-permute-done.2, bf16[2048,2048]{1,0:T(8,128)(2,1)} %collective-permute-done.3, pred[]{:T(512)S(6)} %eq.2), kind=kLoop, calls=%fused_computation.20 | loop fusion | flops 8388608 | bytes 33554432 | tf_op jit(solution)/shard_map/jit(_where)/select_n | solution.py:47
  496.9 90.5 %fusion.8 = f32[2048,4096]{1,0:T(8,128)} fusion(f32[2048,4096]{1,0:T(8,128)} %fusion.6, bf16[8192,4096]{1,0:T(8,128)(2,1)} %param.5, s32[]{:T(128)S(6)} %mul.8, bf16[2048,2048]{1,0:T(8,128)(2,1)} %get-tuple-element.11, bf16[2048,2048]{1,0:T(8,128)(2,1)} %get-tuple-element.10), kind=kOutput, calls=%fused_computation.8 | convolution fusion | flops 68761419776 | bytes 117440512 | tf_op jit(solution)/shard_map/dot_general | solution.py:65
  587.4 1.3 slice_add_fusion.4
  588.7 0.0 collective-permute-start.4
  588.7 57.1 %collective-permute-done.7 = f32[32,2048]{1,0:T(8,128)} collective-permute-done((f32[32,2048]{1,0:T(8,128)}, f32[32,2048]{1,0:T(8,128)}, u32[]{:S(2)}, u32[]{:S(2)}) %collective-permute-start.7) | collective-permute-done | bytes 262176 | tf_op jit(solution)/shard_map/ppermute | solution.py:41
  645.8 0.9 slice.56
  646.8 1.3 collective-permute-start.8
  648.1 0.0 collective-permute-done.5
  648.1 11.6 %dynamic-slice_add_fusion = f32[2048,2048]{1,0:T(8,128)S(1)} fusion(f32[2048,2048]{1,0:T(8,128)} %collective-permute-done.5, f32[4096,2048]{1,0:T(8,128)} %fusion.4, s32[]{:T(128)S(6)} %mul.9), kind=kLoop, calls=%fused_computation.15 | loop fusion | flops 4194304 | bytes 50331652 | tf_op jit(solution)/shard_map/add | solution.py:90
  659.7 0.0 copy-start
  659.8 0.0 collective-permute-done.8
  659.8 5.7 copy-done
  665.5 0.9 fusion.22
  666.4 4.5 dynamic_update_slice.9
  670.9 0.0 collective-permute-done.9
  670.9 12.0 %fusion.18 = bf16[2048,2048]{1,0:T(8,128)(2,1)} fusion(bf16[2048,2048]{1,0:T(8,128)(2,1)} %dynamic_update_slice.9, f32[1600,2048]{1,0:T(8,128)} %collective-permute-done.9, f32[2048,2048]{1,0:T(8,128)} %copy-done), kind=kLoop, calls=%fused_computation.23 | loop fusion | flops 6553600 | bytes 32768000 | tf_op jit(solution)/shard_map/dynamic_update_slice | solution.py:106
  682.9 0.0 collective-permute-done.10
  682.9 4.3 fusion.20._
  687.2 0.0 collective-permute-done.4.part_ref
  687.2 0.8 add_rows.1
  (1 shorter events, 0.0 us)
Async XLA Ops:
  91.4 195.8 %collective-permute-start = (f32[2048,2048]{1,0:T(8,128)}, f32[2048,2048]{1,0:T(8,128)}, u32[]{:S(2)}, u32[]{:S(2)}) collective-permute-start(f32[2048,2048]{1,0:T(8,128)} %constant_dynamic-slice_fusion.1), channel_id=1, source_target_pairs={{0,1},{1,0},{2,3},{3,2},{4,5},{5,4},{6,7},{7,6}} | collective-permute-start | bytes 50331656 | tf_op jit(solution)/shard_map/ppermute | solution.py:41
  91.4 183.8 %collective-permute-start.2 = (bf16[2048,2048]{1,0:T(8,128)(2,1)}, bf16[2048,2048]{1,0:T(8,128)(2,1)}, u32[]{:S(2)}, u32[]{:S(2)}) collective-permute-start(bf16[2048,2048]{1,0:T(8,128)(2,1)} %param.3), channel_id=1, source_target_pairs={{0,2},{1,3},{2,0},{3,1},{4,6},{5,7},{6,4},{7,5}} | collective-permute-start | bytes 25165832 | tf_op jit(solution)/shard_map/ppermute | solution.py:41
  94.0 181.7 %collective-permute-start.1 = (bf16[2048,2048]{1,0:T(8,128)(2,1)}, bf16[2048,2048]{1,0:T(8,128)(2,1)}, u32[]{:S(2)}, u32[]{:S(2)}) collective-permute-start(bf16[2048,2048]{1,0:T(8,128)(2,1)} %param.3), channel_id=1, source_target_pairs={{0,1},{1,0},{2,3},{3,2},{4,5},{5,4},{6,7},{7,6}} | collective-permute-start | bytes 25165832 | tf_op jit(solution)/shard_map/ppermute | solution.py:41
  95.2 213.5 %collective-permute-start.6 = (f32[16,2048]{1,0:T(8,128)S(1)}, f32[16,2048]{1,0:T(8,128)S(1)}, u32[]{:S(2)}, u32[]{:S(2)}) collective-permute-start(f32[16,2048]{1,0:T(8,128)S(1)} %slice.53), channel_id=1, source_target_pairs={{0,1},{2,3},{4,5},{6,7}} | collective-permute-start | bytes 393224 | tf_op jit(solution)/shard_map/ppermute | solution.py:41
  275.2 210.3 %collective-permute-start.3 = (bf16[2048,2048]{1,0:T(8,128)(2,1)}, bf16[2048,2048]{1,0:T(8,128)(2,1)}, u32[]{:S(2)}, u32[]{:S(2)}) collective-permute-start(bf16[2048,2048]{1,0:T(8,128)(2,1)} %collective-permute-done.2), channel_id=1, source_target_pairs={{0,1},{1,0},{2,3},{3,2},{4,5},{5,4},{6,7},{7,6}} | collective-permute-start | bytes 25165832 | tf_op jit(solution)/shard_map/ppermute | solution.py:41
  292.3 390.6 %collective-permute-start.10 = (f32[368,2048]{1,0:T(8,128)}, f32[368,2048]{1,0:T(8,128)}, u32[]{:S(2)}, u32[]{:S(2)}) collective-permute-start(f32[368,2048]{1,0:T(8,128)} %slice_add_fusion.3), channel_id=1, source_target_pairs={{0,2},{1,3},{2,0},{3,1},{4,6},{5,7},{6,4},{7,5}} | collective-permute-start | bytes 9043976 | tf_op jit(solution)/shard_map/ppermute | solution.py:41
  308.7 362.2 %collective-permute-start.9 = (f32[1600,2048]{1,0:T(8,128)}, f32[1600,2048]{1,0:T(8,128)}, u32[]{:S(2)}, u32[]{:S(2)}) collective-permute-start(f32[1600,2048]{1,0:T(8,128)} %slice_add_fusion.1), channel_id=1, source_target_pairs={{0,2},{1,3},{2,0},{3,1},{4,6},{5,7},{6,4},{7,5}} | collective-permute-start | bytes 39321608 | tf_op jit(solution)/shard_map/ppermute | solution.py:41
  310.5 335.3 %collective-permute-start.7 = (f32[32,2048]{1,0:T(8,128)}, f32[32,2048]{1,0:T(8,128)}, u32[]{:S(2)}, u32[]{:S(2)}) collective-permute-start(f32[32,2048]{1,0:T(8,128)} %pad_maximum_fusion), channel_id=1, source_target_pairs={{1,3},{3,1},{5,7},{7,5}} | collective-permute-start | bytes 786440 | tf_op jit(solution)/shard_map/ppermute | solution.py:41
  404.7 243.4 %collective-permute-start.5 = (f32[2048,2048]{1,0:T(8,128)}, f32[2048,2048]{1,0:T(8,128)}, u32[]{:S(2)}, u32[]{:S(2)}) collective-permute-start(f32[2048,2048]{1,0:T(8,128)} %constant_dynamic-slice_fusion), channel_id=1, source_target_pairs={{0,1},{1,0},{2,3},{3,2},{4,5},{5,4},{6,7},{7,6}} | collective-permute-start | bytes 50331656 | tf_op jit(solution)/shard_map/ppermute | solution.py:41
  588.7 98.6 %collective-permute-start.4 = (f32[64,2048]{1,0:T(8,128)S(1)}, f32[64,2048]{1,0:T(8,128)S(1)}, u32[]{:S(2)}, u32[]{:S(2)}) collective-permute-start(f32[64,2048]{1,0:T(8,128)S(1)} %slice_add_fusion.4), channel_id=1, source_target_pairs={{0,2},{1,3},{2,0},{3,1},{4,6},{5,7},{6,4},{7,5}} | collective-permute-start | bytes 1572872 | tf_op jit(solution)/shard_map/ppermute | solution.py:41
  646.8 13.0 %collective-permute-start.8 = (f32[16,2048]{1,0:T(8,128)S(1)}, f32[16,2048]{1,0:T(8,128)S(1)}, u32[]{:S(2)}, u32[]{:S(2)}) collective-permute-start(f32[16,2048]{1,0:T(8,128)S(1)} %slice.56), channel_id=1, source_target_pairs={{1,0},{3,2},{5,4},{7,6}} | collective-permute-start | bytes 393224 | tf_op jit(solution)/shard_map/ppermute | solution.py:41
  659.7 5.7 copy-start

commit v5 on v4

--- a/solution.py
+++ b/solution.py
@@ -6,25 +6,31 @@
 from jax.sharding import PartitionSpec as P
 
 
-CHUNKS = (1600, 368, 64)
+CHUNKS = (1552, 432, 48)
 EXTRA = 16
+PIECE = 16
 
 
 def add_rows(start, part, own, grad_x):
     size = part.shape[0]
 
-    def kernel(part_ref, own_ref, _, out_ref, total, sem):
-        total[...] = (own_ref[...] + part_ref[...]).astype(total.dtype)
-        copy = pltpu.make_async_copy(total, out_ref.at[pl.ds(start, size)], sem)
-        copy.start()
-        copy.wait()
+    def kernel(part_ref, own_ref, _, out_ref, total, sems):
+        copies = []
+        for i in range(size // PIECE):
+            rows = pl.ds(i * PIECE, PIECE)
+            total[rows] = (own_ref[rows] + part_ref[rows]).astype(total.dtype)
+            copies.append(pltpu.make_async_copy(
+                total.at[rows], out_ref.at[pl.ds(start + i * PIECE, PIECE)], sems.at[i]))
+            copies[-1].start()
+        for copy in copies:
+            copy.wait()
 
     return pl.pallas_call(
         kernel,
         out_shape=jax.ShapeDtypeStruct(grad_x.shape, grad_x.dtype),
         in_specs=[pl.BlockSpec(memory_space=pltpu.VMEM)] * 2 + [pl.BlockSpec(memory_space=pl.ANY)],
         out_specs=pl.BlockSpec(memory_space=pl.ANY),
-        scratch_shapes=[pltpu.VMEM(part.shape, grad_x.dtype), pltpu.SemaphoreType.DMA],
+        scratch_shapes=[pltpu.VMEM(part.shape, grad_x.dtype), pltpu.SemaphoreType.DMA((size // PIECE,))],
         input_output_aliases={2: 0},
         cost_estimate=pl.CostEstimate(flops=part.size, bytes_accessed=10 * part.size, transcendentals=0),
         name="add_rows",
@@ -95,8 +101,8 @@
 
         final, grad_w = lax.optimization_barrier((sums[-1], grad_w))
         arrived.append(permute(final, peer_perm))
-        to_core0 = permute(last[:EXTRA], [(t, t ^ 1) for t in core1])
-        arrived.insert(0, jnp.where(core == 0, to_core0, last[EXTRA:]))
+        to_core0 = permute(last, [(t, t ^ 1) for t in core1])
+        arrived.insert(0, jnp.where(core == 0, to_core0[:EXTRA], last[EXTRA:]))
         grad_x, start = jnp.zeros(x_blk.shape, jnp.bfloat16), rows - EXTRA
         for size, part in zip((EXTRA,) + CHUNKS, arrived):
             if part is arrived[-1]:

time: 688 us -> 691 us (level)
  no operation moved by 1% of the time
where the time goes in v5:
time: 691 us
  matrix products  329 us (48%)
  waiting for transfers between devices  239 us (35%)
  other arithmetic  75.1 us (11%)
  local copies, waits for them, and re-layouts  34.5 us (5%)
  starting transfers between devices  11.1 us (2%)
    ppermute x11, waiting for transfers between devices, permute(): return lax.ppermute(value, 'tp', perm)  239 us
    dot_general x2, matrix products, weight_term(): lax.dot_general(x_rows, chip_rows(grad, which), (((0,), (0,)), ((), ())),...  171 us
    dot_general x2, matrix products, partial(): lax.dot_general(chip_rows(grad, which), w_blk, (((1,), (1,)), ((), ())),...  158 us
    dynamic_slice x2, local copies, waits for them, and re-layouts, half(): lax.dynamic_slice_in_dim(value, core * rows, rows, 0, allow_negative_indi...  23.4 us
    select_n x2, other arithmetic, pair(): first = jnp.where(core == 0, mine, other)  22.9 us
    add x3, other arithmetic, per_device(): sums.append(mine + from_sib[start:start + size])  21.5 us
    dynamic_update_slice x2, other arithmetic, per_device(): grad_x = lax.dynamic_update_slice_in_dim(grad_x, done, start, 0)  16.4 us
  transfers between devices with their start and end apart: 11, of which 2 were waited for; matrix products, arithmetic and copies ran while one was open for 50% of the time, Pallas kernels for 0%

profile of v5, /device:TPU:1, one launch (start us, length us, event | category | flops | bytes accessed | tf_op | source)
XLA Modules:
  0.0 690.8 jit_solution(9697663277761490596)
XLA Ops:
  0.6 79.0 %fusion.2 = f32[4096,2048]{1,0:T(8,128)} fusion(bf16[2048,4096]{1,0:T(8,128)(2,1)} %param.4, bf16[8192,4096]{1,0:T(8,128)(2,1)} %param.5, s32[]{:T(128)S(6)} %mul.8), kind=kOutput, calls=%fused_computation.2 | convolution fusion | flops 68719476736 | bytes 83886080 | tf_op jit(solution)/shard_map/dot_general | solution.py:66
  79.6 11.8 %constant_dynamic-slice_fusion.1 = f32[2048,2048]{1,0:T(8,128)} fusion(f32[4096,2048]{1,0:T(8,128)} %fusion.2, s32[]{:T(128)S(6)} %mul.10), kind=kLoop, calls=%fused_computation.38 | loop fusion | bytes 33554436 | tf_op jit(solution)/shard_map/dynamic_slice | solution.py:50
  91.4 0.0 collective-permute-start
  91.4 2.6 collective-permute-start.2
  94.0 0.3 collective-permute-start.1
  94.3 0.9 slice.53
  95.2 1.3 collective-permute-start.6
  96.5 178.6 %collective-permute-done.2 = bf16[2048,2048]{1,0:T(8,128)(2,1)} collective-permute-done((bf16[2048,2048]{1,0:T(8,128)(2,1)}, bf16[2048,2048]{1,0:T(8,128)(2,1)}, u32[]{:S(2)}, u32[]{:S(2)}) %collective-permute-start.2) | collective-permute-done | bytes 8388640 | tf_op jit(solution)/shard_map/ppermute | solution.py:47
  275.2 0.6 collective-permute-start.3
  275.8 0.0 collective-permute-done.1
  275.8 11.4 %broadcast_select_fusion.3 = (bf16[2048,2048]{1,0:T(8,128)(2,1)}, bf16[2048,2048]{1,0:T(8,128)(2,1)}) fusion(bf16[2048,2048]{1,0:T(8,128)(2,1)} %param.3, bf16[2048,2048]{1,0:T(8,128)(2,1)} %collective-permute-done.1, pred[]{:T(512)S(6)} %eq.2), kind=kLoop, calls=%fused_computation.22 | loop fusion | flops 8388608 | bytes 33554432 | tf_op jit(solution)/shard_map/jit(_where)/select_n | solution.py:53
  287.2 0.0 collective-permute-done
  287.2 5.8 slice_add_fusion.3
  292.9 1.5 collective-permute-start.10
  294.4 14.5 %slice_add_fusion.1 = f32[1552,2048]{1,0:T(8,128)} fusion(f32[2048,2048]{1,0:T(8,128)} %collective-permute-done, f32[4096,2048]{1,0:T(8,128)} %fusion.2, s32[]{:T(128)S(6)} %mul.9), kind=kLoop, calls=%fused_computation.18 | loop fusion | flops 3178496 | bytes 38141956 | tf_op jit(solution)/shard_map/add | solution.py:84
  309.0 0.0 collective-permute-start.9
  309.0 0.0 collective-permute-done.6
  309.0 1.1 slice_add_fusion.6
  310.0 0.7 pad_maximum_fusion
  310.7 3.5 collective-permute-start.7
  314.3 78.9 %fusion.4 = f32[4096,2048]{1,0:T(8,128)} fusion(bf16[2048,4096]{1,0:T(8,128)(2,1)} %param.4, bf16[8192,4096]{1,0:T(8,128)(2,1)} %param.5, s32[]{:T(128)S(6)} %mul.11), kind=kOutput, calls=%fused_computation.4 | convolution fusion | flops 68719476736 | bytes 83886080 | tf_op jit(solution)/shard_map/dot_general | solution.py:66
  393.2 11.6 %constant_dynamic-slice_fusion = f32[2048,2048]{1,0:T(8,128)} fusion(f32[4096,2048]{1,0:T(8,128)} %fusion.4, s32[]{:T(128)S(6)} %mul.10), kind=kLoop, calls=%fused_computation.35 | loop fusion | bytes 33554436 | tf_op jit(solution)/shard_map/dynamic_slice | solution.py:50
  404.8 0.0 collective-permute-start.5
  404.8 80.9 %fusion.6 = f32[2048,4096]{1,0:T(8,128)} fusion(bf16[8192,4096]{1,0:T(8,128)(2,1)} %param.5, s32[]{:T(128)S(6)} %mul.11, bf16[2048,2048]{1,0:T(8,128)(2,1)} %get-tuple-element.13, bf16[2048,2048]{1,0:T(8,128)(2,1)} %get-tuple-element.12), kind=kOutput, calls=%fused_computation.6 | convolution fusion | flops 68753031168 | bytes 83886080 | tf_op jit(solution)/shard_map/dot_general | solution.py:71
  485.7 0.0 collective-permute-done.3
  485.7 11.4 %broadcast_select_fusion.1 = (bf16[2048,2048]{1,0:T(8,128)(2,1)}, bf16[2048,2048]{1,0:T(8,128)(2,1)}) fusion(bf16[2048,2048]{1,0:T(8,128)(2,1)} %collective-permute-done.2, bf16[2048,2048]{1,0:T(8,128)(2,1)} %collective-permute-done.3, pred[]{:T(512)S(6)} %eq.2), kind=kLoop, calls=%fused_computation.20 | loop fusion | flops 8388608 | bytes 33554432 | tf_op jit(solution)/shard_map/jit(_where)/select_n | solution.py:53
  497.1 90.5 %fusion.8 = f32[2048,4096]{1,0:T(8,128)} fusion(f32[2048,4096]{1,0:T(8,128)} %fusion.6, bf16[8192,4096]{1,0:T(8,128)(2,1)} %param.5, s32[]{:T(128)S(6)} %mul.8, bf16[2048,2048]{1,0:T(8,128)(2,1)} %get-tuple-element.11, bf16[2048,2048]{1,0:T(8,128)(2,1)} %get-tuple-element.10), kind=kOutput, calls=%fused_computation.8 | convolution fusion | flops 68761419776 | bytes 117440512 | tf_op jit(solution)/shard_map/dot_general | solution.py:71
  587.6 1.2 slice_add_fusion.4
  588.7 0.0 collective-permute-start.4
  588.8 60.5 %collective-permute-done.7 = f32[32,2048]{1,0:T(8,128)} collective-permute-done((f32[32,2048]{1,0:T(8,128)}, f32[32,2048]{1,0:T(8,128)}, u32[]{:S(2)}, u32[]{:S(2)}) %collective-permute-start.7) | collective-permute-done | bytes 262176 | tf_op jit(solution)/shard_map/ppermute | solution.py:47
  649.3 1.3 collective-permute-start.8
  650.6 0.0 collective-permute-done.5
  650.6 11.6 %dynamic-slice_add_fusion = f32[2048,2048]{1,0:T(8,128)S(1)} fusion(f32[2048,2048]{1,0:T(8,128)} %collective-permute-done.5, f32[4096,2048]{1,0:T(8,128)} %fusion.4, s32[]{:T(128)S(6)} %mul.9), kind=kLoop, calls=%fused_computation.15 | loop fusion | flops 4194304 | bytes 50331652 | tf_op jit(solution)/shard_map/add | solution.py:96
  662.3 0.0 copy-start
  662.3 0.0 collective-permute-done.8
  662.3 5.7 copy-done
  668.0 0.9 fusion.22
  669.0 4.5 dynamic_update_slice.9
  673.4 0.0 collective-permute-done.9
  673.4 11.6 %fusion.18 = bf16[2048,2048]{1,0:T(8,128)(2,1)} fusion(bf16[2048,2048]{1,0:T(8,128)(2,1)} %dynamic_update_slice.9, f32[1552,2048]{1,0:T(8,128)} %collective-permute-done.9, f32[2048,2048]{1,0:T(8,128)} %copy-done), kind=kLoop, calls=%fused_computation.23 | loop fusion | flops 6356992 | bytes 31784960 | tf_op jit(solution)/shard_map/dynamic_update_slice | solution.py:112
  685.1 0.0 collective-permute-done.10
  685.1 4.8 fusion.20._
  689.9 0.0 collective-permute-done.4.part_ref
  689.9 0.7 add_rows.1
  (1 shorter events, 0.0 us)
Async XLA Ops:
  91.4 195.8 %collective-permute-start = (f32[2048,2048]{1,0:T(8,128)}, f32[2048,2048]{1,0:T(8,128)}, u32[]{:S(2)}, u32[]{:S(2)}) collective-permute-start(f32[2048,2048]{1,0:T(8,128)} %constant_dynamic-slice_fusion.1), channel_id=1, source_target_pairs={{0,1},{1,0},{2,3},{3,2},{4,5},{5,4},{6,7},{7,6}} | collective-permute-start | bytes 50331656 | tf_op jit(solution)/shard_map/ppermute | solution.py:47
  91.4 183.8 %collective-permute-start.2 = (bf16[2048,2048]{1,0:T(8,128)(2,1)}, bf16[2048,2048]{1,0:T(8,128)(2,1)}, u32[]{:S(2)}, u32[]{:S(2)}) collective-permute-start(bf16[2048,2048]{1,0:T(8,128)(2,1)} %param.3), channel_id=1, source_target_pairs={{0,2},{1,3},{2,0},{3,1},{4,6},{5,7},{6,4},{7,5}} | collective-permute-start | bytes 25165832 | tf_op jit(solution)/shard_map/ppermute | solution.py:47
  94.0 181.7 %collective-permute-start.1 = (bf16[2048,2048]{1,0:T(8,128)(2,1)}, bf16[2048,2048]{1,0:T(8,128)(2,1)}, u32[]{:S(2)}, u32[]{:S(2)}) collective-permute-start(bf16[2048,2048]{1,0:T(8,128)(2,1)} %param.3), channel_id=1, source_target_pairs={{0,1},{1,0},{2,3},{3,2},{4,5},{5,4},{6,7},{7,6}} | collective-permute-start | bytes 25165832 | tf_op jit(solution)/shard_map/ppermute | solution.py:47
  95.2 213.7 %collective-permute-start.6 = (f32[16,2048]{1,0:T(8,128)S(1)}, f32[16,2048]{1,0:T(8,128)S(1)}, u32[]{:S(2)}, u32[]{:S(2)}) collective-permute-start(f32[16,2048]{1,0:T(8,128)S(1)} %slice.53), channel_id=1, source_target_pairs={{0,1},{2,3},{4,5},{6,7}} | collective-permute-start | bytes 393224 | tf_op jit(solution)/shard_map/ppermute | solution.py:47
  275.2 210.5 %collective-permute-start.3 = (bf16[2048,2048]{1,0:T(8,128)(2,1)}, bf16[2048,2048]{1,0:T(8,128)(2,1)}, u32[]{:S(2)}, u32[]{:S(2)}) collective-permute-start(bf16[2048,2048]{1,0:T(8,128)(2,1)} %collective-permute-done.2), channel_id=1, source_target_pairs={{0,1},{1,0},{2,3},{3,2},{4,5},{5,4},{6,7},{7,6}} | collective-permute-start | bytes 25165832 | tf_op jit(solution)/shard_map/ppermute | solution.py:47
  292.9 392.1 %collective-permute-start.10 = (f32[432,2048]{1,0:T(8,128)}, f32[432,2048]{1,0:T(8,128)}, u32[]{:S(2)}, u32[]{:S(2)}) collective-permute-start(f32[432,2048]{1,0:T(8,128)} %slice_add_fusion.3), channel_id=1, source_target_pairs={{0,2},{1,3},{2,0},{3,1},{4,6},{5,7},{6,4},{7,5}} | collective-permute-start | bytes 10616840 | tf_op jit(solution)/shard_map/ppermute | solution.py:47
  309.0 364.5 %collective-permute-start.9 = (f32[1552,2048]{1,0:T(8,128)}, f32[1552,2048]{1,0:T(8,128)}, u32[]{:S(2)}, u32[]{:S(2)}) collective-permute-start(f32[1552,2048]{1,0:T(8,128)} %slice_add_fusion.1), channel_id=1, source_target_pairs={{0,2},{1,3},{2,0},{3,1},{4,6},{5,7},{6,4},{7,5}} | collective-permute-start | bytes 38141960 | tf_op jit(solution)/shard_map/ppermute | solution.py:47
  310.7 338.6 %collective-permute-start.7 = (f32[32,2048]{1,0:T(8,128)}, f32[32,2048]{1,0:T(8,128)}, u32[]{:S(2)}, u32[]{:S(2)}) collective-permute-start(f32[32,2048]{1,0:T(8,128)} %pad_maximum_fusion), channel_id=1, source_target_pairs={{1,3},{3,1},{5,7},{7,5}} | collective-permute-start | bytes 786440 | tf_op jit(solution)/shard_map/ppermute | solution.py:47
  404.8 245.8 %collective-permute-start.5 = (f32[2048,2048]{1,0:T(8,128)}, f32[2048,2048]{1,0:T(8,128)}, u32[]{:S(2)}, u32[]{:S(2)}) collective-permute-start(f32[2048,2048]{1,0:T(8,128)} %constant_dynamic-slice_fusion), channel_id=1, source_target_pairs={{0,1},{1,0},{2,3},{3,2},{4,5},{5,4},{6,7},{7,6}} | collective-permute-start | bytes 50331656 | tf_op jit(solution)/shard_map/ppermute | solution.py:47
  588.7 101.1 %collective-permute-start.4 = (f32[48,2048]{1,0:T(8,128)S(1)}, f32[48,2048]{1,0:T(8,128)S(1)}, u32[]{:S(2)}, u32[]{:S(2)}) collective-permute-start(f32[48,2048]{1,0:T(8,128)S(1)} %slice_add_fusion.4), channel_id=1, source_target_pairs={{0,2},{1,3},{2,0},{3,1},{4,6},{5,7},{6,4},{7,5}} | collective-permute-start | bytes 1179656 | tf_op jit(solution)/shard_map/ppermute | solution.py:47
  649.3 13.0 %collective-permute-start.8 = (f32[32,2048]{1,0:T(8,128)}, f32[32,2048]{1,0:T(8,128)S(1)}, u32[]{:S(2)}, u32[]{:S(2)}) collective-permute-start(f32[32,2048]{1,0:T(8,128)} %collective-permute-done.7), channel_id=1, source_target_pairs={{1,0},{3,2},{5,4},{7,6}} | collective-permute-start | bytes 786440 | tf_op jit(solution)/shard_map/ppermute | solution.py:47
  662.3 5.7 copy-start
